TPU v7x, 32 devices: a whole 2x2x4 slice. The times are simulated.
32 devices in a mesh: dp: 8 (over z, y), mp: 4 (over x, core).
Axes of the slice: x: 2, y: 2, z: 4, core: 2. Of those that a mesh axis runs over, the one named last changes fastest.
Arguments:
- tokens: bfloat16 [32768, 768], P(('dp', 'mp')), may hold values from -6 to 6
- cotangent: bfloat16 [32768, 768], P(('dp', 'mp')), may hold values from -6 to 6
- prompts: float32 [50, 768], replicated, may hold values from -6 to 6
- segments: int32 [32768], P(('dp', 'mp')), may hold values from 0 to 6, as said below
- prompt_slot_index: int32 [32768], P(('dp', 'mp')), may hold values from 0 to 50, as said below
- norm_gain: float32 [2, 768], replicated, may hold values from 0.5 to 1.5
- norm_shift: float32 [2, 768], replicated, may hold values from -2 to 2
- attn_qkv: bfloat16 [3, 768, 768], P(None, ('dp', 'mp')), may hold values from -0.21875 to 0.21875
- attn_bias: float32 [3, 768], replicated, may hold values from -2 to 2
- attn_out: bfloat16 [768, 768], P(('dp', 'mp')), may hold values from -0.625 to 0.625
- mlp_weight: bfloat16 [2, 768, 3072], P(None, 'dp', 'mp'), may hold values from -0.21875 to 0.21875
- mlp_bias_up: float32 [3072], replicated, may hold values from -2 to 2
- mlp_bias_down: float32 [768], replicated, may hold values from -2 to 2
Outputs:
- block_output: bfloat16 [32768, 768], P(('dp', 'mp'))
- input_grad: float32 [32768, 768], P(('dp', 'mp'))
- prompt_grad: float32 [50, 768], replicated
- gain_grad: float32 [2, 768], replicated
- shift_grad: float32 [2, 768], replicated
- qkv_grad: float32 [3, 768, 768], P(None, ('dp', 'mp'))
- attn_bias_grad: float32 [3, 768], replicated
- attn_out_grad: float32 [768, 768], P(('dp', 'mp'))
- mlp_grad: float32 [2, 768, 3072], P(None, 'dp', 'mp')
- up_bias_grad: float32 [3072], replicated
- down_bias_grad: float32 [768], replicated
Inputs may be any that keep to these rules, and one draw needn't show every extreme that they name: Every packed row holds images of one size: from the row's start, as many whole segments of 151, of 247 or of 627 tokens as fit, numbered from 0, then one segment of the remaining tokens. Row 0 holds the smallest images. `prompt_slot_index`: in each image segment, tokens 1 to 50 carry slots 0 to 49; all other tokens carry 50.
All inputs are finite; a program needn't handle non-finite values.
Results may differ from a plain program's by a relative error of at most 0.014.
Values may be sent and summed in bfloat16 or wider, within the bound.
No kernel may reach another device: no remote copies, remote signals or barrier semaphores. Data moves between devices by JAX's collectives and lax.ppermute only.
A program may use at most 256 MiB of HBM per device.

v0:
```python
from functools import partial
import jax
import jax.numpy as jnp
from jax import lax
from jax.sharding import PartitionSpec as P

HEAD_SIZE = 64
NPROMPT = 50
PACKED_ROW_LENGTH = 1024
EPS = 1e-06
HIGHEST = lax.Precision.HIGHEST
MASKED = -1e30


def layer_norm(value_list, gain_row, shift_row):
    centre = jnp.mean(value_list, axis=-1, keepdims=True)
    centred = value_list - centre
    spread = jnp.mean(centred * centred, axis=-1, keepdims=True)
    return centred * lax.rsqrt(spread + EPS) * gain_row + shift_row


def gelu_exact(value_list):
    return jax.nn.gelu(value_list, approximate=False)


def masked_scores(query_tile, key_heads, seg_tile, seg_row, factor):
    scores = (
        jnp.einsum("qhd,khd->hqk", query_tile, key_heads, preferred_element_type=jnp.float32)
        * factor
    )
    allowed = seg_tile[:, None] == seg_row[None, :]
    return jnp.where(allowed[None], scores, MASKED)


def attend_forward(packed, tile_row_list):
    query_heads, key_heads, value_heads, seg_row = packed
    factor = query_heads.shape[2] ** (-0.5)

    def one_tile(tile_number):
        first_row = tile_number * tile_row_list
        query_tile = lax.dynamic_slice_in_dim(query_heads, first_row, tile_row_list, 0)
        seg_tile = lax.dynamic_slice_in_dim(seg_row, first_row, tile_row_list, 0)
        scores = masked_scores(query_tile, key_heads, seg_tile, seg_row, factor)
        row_peak = jnp.max(scores, axis=-1, keepdims=True)
        raised = jnp.exp(scores - row_peak)
        totals_row = jnp.sum(raised, axis=-1, keepdims=True)
        weights = (raised / totals_row).astype(jnp.bfloat16)
        mixed = jnp.einsum("hqk,khd->qhd", weights, value_heads, preferred_element_type=jnp.float32)
        return (mixed.astype(jnp.bfloat16), (row_peak + jnp.log(totals_row))[:, :, 0])

    return lax.map(one_tile, jnp.arange(query_heads.shape[0] // tile_row_list))


def attend_backward(packed, tile_row_list):
    query_heads, key_heads, value_heads, seg_row, log_sums, grad_heads = packed
    length, head_count, head_width = key_heads.shape
    factor = head_width ** (-0.5)

    def one_tile(running, tile_number):
        grad_keys, grad_values = running
        first_row = tile_number * tile_row_list
        query_tile = lax.dynamic_slice_in_dim(query_heads, first_row, tile_row_list, 0)
        seg_tile = lax.dynamic_slice_in_dim(seg_row, first_row, tile_row_list, 0)
        grad_tile = lax.dynamic_slice_in_dim(grad_heads, first_row, tile_row_list, 0)
        scores = masked_scores(query_tile, key_heads, seg_tile, seg_row, factor)
        weights = jnp.exp(scores - log_sums[tile_number][:, :, None])
        grad_weights = jnp.einsum(
            "qhd,khd->hqk", grad_tile, value_heads, preferred_element_type=jnp.float32
        )
        weighted = jnp.sum(weights * grad_weights, axis=-1, keepdims=True)
        grad_scores = (weights * (grad_weights - weighted)).astype(jnp.bfloat16)
        grad_query = (
            jnp.einsum("hqk,khd->qhd", grad_scores, key_heads, preferred_element_type=jnp.float32)
            * factor
        )
        grad_keys = (
            grad_keys
            + jnp.einsum(
                "hqk,qhd->khd", grad_scores, query_tile, preferred_element_type=jnp.float32
            )
            * factor
        )
        grad_values = grad_values + jnp.einsum(
            "hqk,qhd->khd",
            weights.astype(jnp.bfloat16),
            grad_tile,
            preferred_element_type=jnp.float32,
        )
        return ((grad_keys, grad_values), grad_query)

    zeros_heads = jnp.zeros((length, head_count, head_width), jnp.float32)
    (grad_keys, grad_values), grad_queries = lax.scan(
        one_tile, (zeros_heads, zeros_heads), jnp.arange(length // tile_row_list)
    )
    return (grad_queries.reshape(length, head_count, head_width), grad_keys, grad_values)


def split_heads(value_list, row_count_total):
    return value_list.reshape(row_count_total, PACKED_ROW_LENGTH, -1, HEAD_SIZE)


def local(
    tokens,
    cotangent,
    prompts,
    segments,
    prompt_slot_index,
    norm_gain,
    norm_shift,
    attn_qkv,
    attn_bias,
    attn_out,
    mlp_weight,
    mlp_bias_up,
    mlp_bias_down,
):
    token_tally = tokens.shape[0]
    feature_count = tokens.shape[1]
    row_count_total = token_tally // PACKED_ROW_LENGTH
    tile_row_list = min(512, PACKED_ROW_LENGTH)
    qkv_all, out_all = (
        lax.all_gather(attn_qkv, ("dp", "mp"), axis=1, tiled=True),
        lax.all_gather(attn_out, ("dp", "mp"), axis=0, tiled=True),
    )
    mlp_part = lax.all_gather(mlp_weight, "dp", axis=1, tiled=True)
    input_list = tokens.astype(jnp.float32)
    prompt_table = jnp.concatenate([prompts, jnp.zeros((1, feature_count), jnp.float32)], 0)
    onehot = (
        prompt_slot_index[:, None] == jnp.arange(NPROMPT + 1, dtype=jnp.int32)[None, :]
    ).astype(jnp.float32)
    is_prompt = (prompt_slot_index < NPROMPT)[:, None]
    start = jnp.where(is_prompt, jnp.dot(onehot, prompt_table, precision=HIGHEST), input_list)
    normed_one = layer_norm(start, norm_gain[0], norm_shift[0]).astype(jnp.bfloat16)
    projected = jnp.einsum("td,cde->cte", normed_one, qkv_all, preferred_element_type=jnp.float32)
    queries = (projected[0] + attn_bias[0]).astype(jnp.bfloat16)
    key_rows = projected[1].astype(jnp.bfloat16)
    value_rows = (projected[2] + attn_bias[1]).astype(jnp.bfloat16)
    segment_row_list = segments.reshape(row_count_total, PACKED_ROW_LENGTH)
    query_split = split_heads(queries, row_count_total)
    key_split = split_heads(key_rows, row_count_total)
    value_split = split_heads(value_rows, row_count_total)
    mixed, log_sums = lax.map(
        partial(attend_forward, tile_row_list=tile_row_list),
        (query_split, key_split, value_split, segment_row_list),
    )
    mixed = mixed.reshape(token_tally, feature_count)
    middle = start + jnp.dot(mixed, out_all, preferred_element_type=jnp.float32) + attn_bias[2]
    normed_two = layer_norm(middle, norm_gain[1], norm_shift[1]).astype(jnp.bfloat16)
    grad_output = cotangent.astype(jnp.float32)
    grad_down = jnp.sum(grad_output, axis=0)
    gathered = lax.all_gather(normed_two, "mp", axis=0, tiled=True)
    unit_count = mlp_part.shape[2]
    offset = lax.axis_index("mp") * unit_count
    bias_part = lax.dynamic_slice_in_dim(mlp_bias_up, offset, unit_count, 0)
    before = jnp.dot(gathered, mlp_part[0], preferred_element_type=jnp.float32) + bias_part
    hidden = gelu_exact(before).astype(jnp.bfloat16)
    piece = hidden
    branch = lax.psum_scatter(
        jnp.einsum("tf,df->td", piece, mlp_part[1], preferred_element_type=jnp.float32).astype(
            jnp.bfloat16
        ),
        "mp",
        scatter_dimension=0,
        tiled=True,
    ).astype(jnp.float32)
    output = middle + branch + mlp_bias_down
    grad_gathered = lax.all_gather(cotangent, "mp", axis=0, tiled=True)
    grad_hidden = jnp.dot(grad_gathered, mlp_part[1], preferred_element_type=jnp.float32)
    before_out, gelu_pull = jax.vjp(gelu_exact, before)
    grad_before = gelu_pull(grad_hidden)[0].astype(jnp.bfloat16)
    grad_mlp = jnp.stack(
        [
            jnp.einsum("td,tf->df", gathered, grad_before, preferred_element_type=jnp.float32),
            jnp.einsum("td,tf->df", grad_gathered, hidden, preferred_element_type=jnp.float32),
        ]
    )
    grad_up = lax.dynamic_update_slice_in_dim(
        jnp.zeros_like(mlp_bias_up), jnp.sum(grad_before.astype(jnp.float32), axis=0), offset, 0
    )
    piece = grad_before
    grad_normed_two = lax.psum_scatter(
        jnp.einsum("tf,df->td", piece, mlp_part[0], preferred_element_type=jnp.float32).astype(
            jnp.bfloat16
        ),
        "mp",
        scatter_dimension=0,
        tiled=True,
    ).astype(jnp.float32)
    mlp_grad = lax.psum_scatter(grad_mlp, "dp", scatter_dimension=1, tiled=True)
    norm_out_two, pull_two = jax.vjp(layer_norm, middle, norm_gain[1], norm_shift[1])
    grad_from_two, grad_gain_two, grad_shift_two = pull_two(grad_normed_two)
    grad_middle = grad_output + grad_from_two
    grad_branch = grad_middle.astype(jnp.bfloat16)
    grad_bias_out = jnp.sum(grad_branch.astype(jnp.float32), axis=0)
    grad_out_weight = jnp.einsum(
        "td,te->de", mixed, grad_branch, preferred_element_type=jnp.float32
    )
    grad_mixed = jnp.einsum(
        "te,de->td", grad_branch, out_all, preferred_element_type=jnp.float32
    ).astype(jnp.bfloat16)
    grad_queries, grad_keys, grad_values = lax.map(
        partial(attend_backward, tile_row_list=tile_row_list),
        (
            query_split,
            key_split,
            value_split,
            segment_row_list,
            log_sums,
            split_heads(grad_mixed, row_count_total),
        ),
    )
    grad_projected = jnp.stack(
        [
            grad_queries.reshape(token_tally, feature_count),
            grad_keys.reshape(token_tally, feature_count),
            grad_values.reshape(token_tally, feature_count),
        ]
    ).astype(jnp.bfloat16)
    grad_qkv = jnp.einsum(
        "td,cte->cde", normed_one, grad_projected, preferred_element_type=jnp.float32
    )
    grad_attn_bias = jnp.stack(
        [
            jnp.sum(grad_projected[0].astype(jnp.float32), axis=0),
            jnp.sum(grad_projected[2].astype(jnp.float32), axis=0),
            grad_bias_out,
        ]
    )
    grad_normed_one = jnp.einsum(
        "cte,cde->td", grad_projected, qkv_all, preferred_element_type=jnp.float32
    )
    norm_out_one, pull_one = jax.vjp(layer_norm, start, norm_gain[0], norm_shift[0])
    grad_from_one, grad_gain_one, grad_shift_one = pull_one(grad_normed_one)
    grad_start = grad_middle + grad_from_one
    input_grad = jnp.where(is_prompt, 0.0, grad_start)
    grad_prompts = jnp.dot(onehot.T, grad_start, precision=HIGHEST)[:NPROMPT]
    qkv_grad, out_grad = (
        lax.psum_scatter(grad_qkv, ("dp", "mp"), scatter_dimension=1, tiled=True),
        lax.psum_scatter(grad_out_weight, ("dp", "mp"), scatter_dimension=0, tiled=True),
    )
    summed = lax.psum(
        (
            grad_prompts,
            jnp.stack([grad_gain_one, grad_gain_two]),
            jnp.stack([grad_shift_one, grad_shift_two]),
            grad_attn_bias,
            grad_up,
            grad_down,
        ),
        ("dp", "mp"),
    )
    return (
        output.astype(jnp.bfloat16),
        input_grad,
        summed[0],
        summed[1],
        summed[2],
        qkv_grad,
        summed[3],
        out_grad,
        mlp_grad,
        summed[4],
        summed[5],
    )


def solution(mesh):
    return jax.shard_map(
        local,
        mesh=mesh,
        in_specs=(
            P(("dp", "mp"), None),
            P(("dp", "mp"), None),
            P(),
            P(("dp", "mp")),
            P(("dp", "mp")),
            P(),
            P(),
            P(None, ("dp", "mp"), None),
            P(),
            P(("dp", "mp"), None),
            P(None, "dp", "mp"),
            P(),
            P(),
        ),
        out_specs=(
            P(("dp", "mp"), None),
            P(("dp", "mp"), None),
            P(),
            P(),
            P(),
            P(None, ("dp", "mp"), None),
            P(),
            P(("dp", "mp"), None),
            P(None, "dp", "mp"),
            P(),
            P(),
        ),
        check_vma=False,
    )
```

profile of v0, /device:TPU:0, one launch (start us, length us, event | category | flops | bytes accessed | tf_op | source)
XLA Modules:
  0.0 1018.5 jit_solution(4451620781767088363)
XLA Ops:
  14.5 2.6 copy.58
  17.1 3.2 fusion.59
  21.6 52.1 %all-gather.6.cloned.1.call-done = bf16[3,768,768]{2,1,0:T(8,128)(2,1)} async-done(((bf16[3,24,768]{2,1,0:T(8,128)(2,1)}), bf16[3,768,768]{2,1,0:T(8,128)(2,1)}) %all-gather.6.cloned.1.call-update) | async-done | bytes 3538960 | tf_op jit(solution)/shard_map/all_gather | solution.py:122
  73.7 6.2 convolution_bitcast_fusion
  82.9 73.5 %while.47 = (s32[]{:T(128)}, bf16[2,512,12,64]{1,3,2,0:T(8,128)(2,1)}, f32[2,12,512]{2,1,0:T(8,128)S(1)}, s32[2]{0:T(128)S(1)}, s32[1024]{0:T(1024)S(1)}, /*inde...) while((s32[]{:T(128)}, ...), condition=%wide.region_5.6_spmd, body=%wide.region_2.5_spmd.sunk | while | flops 1687021568 | bytes 189499632 | solution.py:51
  85.1 10.6 %fusion.103 = (f32[12,512]{1,0:T(8,128)S(1)}, f32[12,512,1024]{2,1,0:T(8,128)}) fusion(pred[512,1024]{1,0:T(8,128)(4,1)S(1)} %broadcast_compare_fusion.5, bf16[1024,12,64]{0,2,1:T(8,128)(2,1)S(1)} %get-tuple-element.478, bf16[1024,12,64]{0,2,1:T(8,128)(2,1)S(1)} %get-tuple-element.477, s32[]{:T(128)S(6)} %select_n.77), kind=kOutput, calls=%fused_computation.3.clone.1 | convolution fusion | flops 824174592 | bytes 28073988 | tf_op jit(solution)/shard_map/while/body/eval_jaxpr/while/body/eval_jaxpr/qhd,khd->hqk/dot_general | solution.py:28
  95.7 12.3 %fusion.104 = f32[12,512]{1,0:T(8,128)S(1)} fusion(f32[12,512,1024]{2,1,0:T(8,128)} %get-tuple-element.433, f32[12,512]{1,0:T(8,128)S(1)} %get-tuple-element.434, pred[512,1024]{1,0:T(8,128)(4,1)S(1)} %broadcast_compare_fusion.5), kind=kLoop, calls=%fused_computation.4.clone.1 | loop fusion | flops 25159680 | bytes 25739264 | tf_op jit(solution)/shard_map/while/body/eval_jaxpr/while/body/eval_jaxpr/reduce_sum | solution.py:46
  108.1 3.1 copy-done
  111.2 8.5 fusion.105
  121.4 10.7 %fusion.103 = (f32[12,512]{1,0:T(8,128)S(1)}, f32[12,512,1024]{2,1,0:T(8,128)}) fusion(pred[512,1024]{1,0:T(8,128)(4,1)S(1)} %broadcast_compare_fusion.5, bf16[1024,12,64]{0,2,1:T(8,128)(2,1)S(1)} %get-tuple-element.478, bf16[1024,12,64]{0,2,1:T(8,128)(2,1)S(1)} %get-tuple-element.477, s32[]{:T(128)S(6)} %select_n.77), kind=kOutput, calls=%fused_computation.3.clone.1 | convolution fusion | flops 824174592 | bytes 28073988 | tf_op jit(solution)/shard_map/while/body/eval_jaxpr/while/body/eval_jaxpr/qhd,khd->hqk/dot_general | solution.py:28
  132.1 12.4 %fusion.104 = f32[12,512]{1,0:T(8,128)S(1)} fusion(f32[12,512,1024]{2,1,0:T(8,128)} %get-tuple-element.433, f32[12,512]{1,0:T(8,128)S(1)} %get-tuple-element.434, pred[512,1024]{1,0:T(8,128)(4,1)S(1)} %broadcast_compare_fusion.5), kind=kLoop, calls=%fused_computation.4.clone.1 | loop fusion | flops 25159680 | bytes 25739264 | tf_op jit(solution)/shard_map/while/body/eval_jaxpr/while/body/eval_jaxpr/reduce_sum | solution.py:46
  144.5 3.3 copy-done
  147.8 8.5 fusion.105
  156.4 4.2 copy.60
  162.3 4.4 fusion.60
  171.4 10.8 %all-gather.12.cloned.1.call-done = bf16[2,768,768]{2,1,0:T(8,128)(2,1)} async-done(((bf16[2,96,768]{2,1,0:T(8,128)(2,1)}), bf16[2,768,768]{2,1,0:T(8,128)(2,1)}) %all-gather.12.cloned.1.call-update) | async-done | bytes 2359312 | tf_op jit(solution)/shard_map/all_gather | solution.py:125
  182.2 46.9 %all-gather.10.cloned.1.call-done = bf16[4096,768]{0,1:T(8,128)(2,1)} async-done(((bf16[1024,768]{0,1:T(8,128)(2,1)}), bf16[4096,768]{0,1:T(8,128)(2,1)}) %all-gather.10.cloned.1.call-update) | async-done | bytes 6291472 | tf_op jit(solution)/shard_map/all_gather | solution.py:151
  229.1 35.4 %multiply_convert_fusion.1 = (bf16[4096,768]{1,0:T(8,128)(2,1)}, f32[4096,768]{1,0:T(8,128)}, f32[4096,768]{1,0:T(8,128)}) fusion(f32[768]{0:T(1024)S(1)} %dynamic_slice.51, bf16[4096,768]{0,1:T(8,128)(2,1)} %all-gather.10.cloned.1.call-done, bf16[2,768,768]{2,1,0:T(8,128)(2,1)} %all-gather.12.cloned.1.call-done), kind=kOutput, calls=%fused_computation.43 | convolution fusion | flops 5039456256 | bytes 38931456 | tf_op jit(solution)/shard_map/dot_general | solution.py:155
  264.5 12.4 %all-gather.14.cloned.1.call-done = bf16[4096,768]{1,0:T(8,128)(2,1)} async-done(((bf16[1024,768]{1,0:T(8,128)(2,1)}), bf16[4096,768]{1,0:T(8,128)(2,1)}) %all-gather.14.cloned.1.call-update) | async-done | bytes 6291472 | tf_op jit(solution)/shard_map/all_gather | solution.py:167
  276.9 15.2 %convert_reduce_fusion = (f32[768]{0:T(1024)}, bf16[4096,768]{1,0:T(8,128)(2,1)S(1)}) fusion(f32[4096,768]{1,0:T(8,128)} %get-tuple-element.303, bf16[4096,768]{1,0:T(8,128)(2,1)} %all-gather.14.cloned.1.call-done, bf16[2,768,768]{2,1,0:T(8,128)(2,1)S(1)} %copy-done.65, f32[4096,768]{1,0:T(8,128)} %get-tuple-element.317, f32[768]{0:T(1024)S(1)} %dynamic_slice.51), kind=kOutput, calls=%fused_computation.41 | convolution fusion | flops 4885314560 | bytes 38935552 | tf_op jit(solution)/shard_map/dot_general | solution.py:168
  292.1 2.6 copy-done.67
  294.7 6.9 convolution_convert_fusion
  305.6 9.9 convolution_convert_fusion.1
  315.6 44.2 %reduce-scatter.7.cloned.1.call-done = bf16[1024,768]{0,1:T(8,128)(2,1)} async-done(((bf16[4096,768]{0,1:T(8,128)(2,1)}), bf16[1024,768]{0,1:T(8,128)(2,1)}) %reduce-scatter.7.cloned.1.call-update) | async-done | bytes 1572880 | tf_op jit(solution)/shard_map/reduce_scatter | solution.py:181
  359.8 3.1 convert_reduce_fusion.1
  362.9 2.2 fusion.38
  365.1 2.0 convert_reduce_fusion.3
  367.2 2.6 convolution_convert_fusion.2
  369.8 175.1 %while.48 = (s32[]{:T(128)}, f32[1024,12,64]{0,2,1:T(8,128)}, f32[1024,12,64]{0,2,1:T(8,128)}, bf16[2,512,12,64]{1,3,2,0:T(8,128)(2,1)}, s32[2]{0:T(128)S(1)}, /...) while((s32[]{:T(128)}, f32[1024,12,64]{0,2,1:T(8,128)}, ...), condition=%wide.region_14.15_spmd.clone, body=%wide.region_12.14_spmd.clone.sunk | while | flops 4125747200 | bytes 225634640 | solution.py:92
  373.9 12.1 %fusion.115 = f32[12,512,1024]{2,1,0:T(8,128)} fusion(bf16[1024,12,64]{0,2,1:T(8,128)(2,1)S(1)} %get-tuple-element.523, bf16[1024,12,64]{0,2,1:T(8,128)(2,1)} %get-tuple-element.521, s32[]{:T(128)S(6)} %select_n.81), kind=kOutput, calls=%fused_computation.30.clone.1 | convolution fusion | flops 805306368 | bytes 27525124 | tf_op jit(solution)/shard_map/while/body/eval_jaxpr/while/body/eval_jaxpr/qhd,khd->hqk/dot_general | solution.py:28
  386.1 13.3 %bitcast_add_fusion.5 = f32[1024,12,64]{0,2,1:T(8,128)} fusion(f32[1024,12,64]{0,2,1:T(8,128)} %get-tuple-element.502, f32[12,512,1024]{2,1,0:T(8,128)} %fusion.115, f32[12,512]{1,0:T(8,128)S(1)} %dynamic-slice_bitcast_fusion.2, pred[512,1024]{1,0:T(8,128)(4,1)S(1)} %broadcast_compare_fusion.6, pred[]{:T(512)S(6)} %compare.4, ...), kind=kOutput, calls=%fused_computation.22.clone.1 | convolution fusion | flops 832045056 | bytes 32800772 | tf_op jit(solution)/shard_map/while/body/eval_jaxpr/while/body/eval_jaxpr/hqk,qhd->khd/dot_general | solution.py:83
  399.4 18.3 %multiply_reduce_fusion.6 = (f32[12,512]{1,0:T(8,128)S(1)}, f32[12,512,1024]{2,1,0:T(8,128)}) fusion(f32[12,512,1024]{2,1,0:T(8,128)} %fusion.115, f32[12,512]{1,0:T(8,128)S(1)} %dynamic-slice_bitcast_fusion.2, pred[512,1024]{1,0:T(8,128)(4,1)S(1)} %broadcast_compare_fusion.6, bf16[1024,12,64]{0,2,1:T(8,128)(2,1)} %get-tuple-element.526, ...), kind=kOutput, calls=%fused_computation.17.clone.1 | convolution fusion | flops 836757504 | bytes 53264388 | tf_op jit(solution)/shard_map/while/body/eval_jaxpr/while/body/eval_jaxpr/qhd,khd->hqk/dot_general | solution.py:67
  417.7 21.4 %multiply_convert_fusion.3 = bf16[12,512,1024]{2,1,0:T(8,128)(2,1)} fusion(f32[12,512,1024]{2,1,0:T(8,128)} %get-tuple-element.446, f32[12,512,1024]{2,1,0:T(8,128)} %fusion.115, f32[12,512]{1,0:T(8,128)S(1)} %get-tuple-element.447, f32[12,512]{1,0:T(8,128)S(1)} %dynamic-slice_bitcast_fusion.2, pred[512,1024]{1,0:T(8,128)(4,1)S(1)} %broadcast_compare_fusion.6), kind=kLoop, calls=%fused_computation.16.clone.1 | loop fusion | flops 37748736 | bytes 63488000 | tf_op jit(solution)/shard_map/while/body/eval_jaxpr/while/body/eval_jaxpr/convert_element_type | solution.py:71
  439.0 9.5 bitcast_dynamic-update-slice_fusion.5
  448.5 8.6 bitcast_add_fusion.4
  460.7 11.5 %fusion.115 = f32[12,512,1024]{2,1,0:T(8,128)} fusion(bf16[1024,12,64]{0,2,1:T(8,128)(2,1)S(1)} %get-tuple-element.523, bf16[1024,12,64]{0,2,1:T(8,128)(2,1)} %get-tuple-element.521, s32[]{:T(128)S(6)} %select_n.81), kind=kOutput, calls=%fused_computation.30.clone.1 | convolution fusion | flops 805306368 | bytes 27525124 | tf_op jit(solution)/shard_map/while/body/eval_jaxpr/while/body/eval_jaxpr/qhd,khd->hqk/dot_general | solution.py:28
  472.2 14.2 %bitcast_add_fusion.5 = f32[1024,12,64]{0,2,1:T(8,128)} fusion(f32[1024,12,64]{0,2,1:T(8,128)} %get-tuple-element.502, f32[12,512,1024]{2,1,0:T(8,128)} %fusion.115, f32[12,512]{1,0:T(8,128)S(1)} %dynamic-slice_bitcast_fusion.2, pred[512,1024]{1,0:T(8,128)(4,1)S(1)} %broadcast_compare_fusion.6, pred[]{:T(512)S(6)} %compare.4, ...), kind=kOutput, calls=%fused_computation.22.clone.1 | convolution fusion | flops 832045056 | bytes 32800772 | tf_op jit(solution)/shard_map/while/body/eval_jaxpr/while/body/eval_jaxpr/hqk,qhd->khd/dot_general | solution.py:83
  486.4 18.1 %multiply_reduce_fusion.6 = (f32[12,512]{1,0:T(8,128)S(1)}, f32[12,512,1024]{2,1,0:T(8,128)}) fusion(f32[12,512,1024]{2,1,0:T(8,128)} %fusion.115, f32[12,512]{1,0:T(8,128)S(1)} %dynamic-slice_bitcast_fusion.2, pred[512,1024]{1,0:T(8,128)(4,1)S(1)} %broadcast_compare_fusion.6, bf16[1024,12,64]{0,2,1:T(8,128)(2,1)} %get-tuple-element.526, ...), kind=kOutput, calls=%fused_computation.17.clone.1 | convolution fusion | flops 836757504 | bytes 53264388 | tf_op jit(solution)/shard_map/while/body/eval_jaxpr/while/body/eval_jaxpr/qhd,khd->hqk/dot_general | solution.py:67
  504.5 21.2 %multiply_convert_fusion.3 = bf16[12,512,1024]{2,1,0:T(8,128)(2,1)} fusion(f32[12,512,1024]{2,1,0:T(8,128)} %get-tuple-element.446, f32[12,512,1024]{2,1,0:T(8,128)} %fusion.115, f32[12,512]{1,0:T(8,128)S(1)} %get-tuple-element.447, f32[12,512]{1,0:T(8,128)S(1)} %dynamic-slice_bitcast_fusion.2, pred[512,1024]{1,0:T(8,128)(4,1)S(1)} %broadcast_compare_fusion.6), kind=kLoop, calls=%fused_computation.16.clone.1 | loop fusion | flops 37748736 | bytes 63488000 | tf_op jit(solution)/shard_map/while/body/eval_jaxpr/while/body/eval_jaxpr/convert_element_type | solution.py:71
  525.8 9.5 bitcast_dynamic-update-slice_fusion.5
  535.3 9.5 bitcast_add_fusion.4
  544.9 4.2 copy.64
  549.1 4.0 stack_reshape.12
  553.1 2.6 copy.65
  557.1 2.6 copy.66
  559.7 3.4 convert_reduce_fusion.4
  563.0 2.6 copy.67
  565.7 9.4 convolution_bitcast_fusion.1
  575.1 11.0 %copy.72 = f32[3,768,768]{2,0,1:T(4,128)} copy(f32[3,768,768]{1,2,0:T(8,128)} %convolution_bitcast_fusion.1) | data formatting | bytes 14155776 | tf_op jit(solution)/shard_map/td,cte->cde/transpose | solution.py:219
  586.1 9.0 fusion.61
  595.1 3.9 copy.68
  599.0 3.0 multiply_reduce_fusion.1
  606.8 3.8 fusion.45
  610.6 9.1 convolution_bitcast_fusion.2
  619.7 9.1 convolution_bitcast_fusion.3
  628.8 2.5 pad_maximum_fusion.1
  631.4 4.8 fusion.62
  636.9 1.7 convert_reduce_fusion.5
  638.6 5.9 broadcast_select_fusion
  644.6 3.7 copy.75
  649.8 41.1 %all-reduce.2 = (f32[2,768]{1,0:T(2,128)}, f32[2,768]{1,0:T(2,128)}, f32[3,768]{1,0:T(4,128)}, f32[3072]{0:T(1024)}, f32[768]{0:T(1024)}) all-reduce(f32[2,768]{1,0:T(2,128)S(1)} %pad_maximum_fusion.7, f32[2,768]{1,0:T(2,128)S(1)} %pad_maximum_fusion.8, ...), channel_id=1, replica_groups=mesh['dp'=8,'mp'=4] {'dp','mp'}, use_global_device_ids=true, to_apply=%region_20.21 | all-reduce | flops 9216 | bytes 73728 | tf_op jit(solution)/shard_map/psum | solution.py:241
  691.0 114.2 %all-reduce.6.cloned.1.call-done = (f32[50,768]{1,0:T(8,128)}, f32[3,768,768]{2,0,1:T(4,128)}) async-done(((f32[50,768]{1,0:T(8,128)}, f32[3,768,768]{2,0,1:T(4,128)}), (f32[50,768]{1,0:T(8,128)}, f32[3,768,768]{2,0,1:T(4,128)})) %all-reduce.6.cloned.1.call-update) | async-done | bytes 7231504 | tf_op jit(solution)/shard_map/psum | solution.py:241
  806.9 98.0 %reduce-scatter.11.cloned.1.call-done = f32[2,96,768]{2,1,0:T(8,128)} async-done(((f32[2,768,768]{2,1,0:T(8,128)}), f32[2,96,768]{2,1,0:T(8,128)}) %reduce-scatter.11.cloned.1.call-update) | async-done | bytes 589840 | tf_op jit(solution)/shard_map/reduce_scatter | solution.py:189
  904.9 104.9 %reduce-scatter.9.cloned.1.call-done = f32[24,768]{1,0:T(8,128)} async-done(((f32[768,768]{1,0:T(8,128)}), f32[24,768]{1,0:T(8,128)}) %reduce-scatter.9.cloned.1.call-update) | async-done | bytes 73744 | tf_op jit(solution)/shard_map/reduce_scatter | solution.py:239
  (228 shorter events, 37.8 us)
Async XLA Ops:
  7.2 9.9 copy-start.50
  7.2 9.9 copy-start.30
  7.2 66.5 %all-gather.6.cloned.1.call-start = ((), (), s32[]{:S(2)}) async-start(), calls=%async_computation.4 | async-start | bytes 3649536 | tf_op jit(solution)/shard_map/all_gather | solution.py:122
  7.9 154.3 %all-gather.8.cloned.1.call-start = ((), (), s32[]{:S(2)}) async-start(), calls=%async_computation.5 | async-start | bytes 1216512 | tf_op jit(solution)/shard_map/all_gather | solution.py:123
  8.7 173.5 %all-gather.12.cloned.1.call-start = ((), (), s32[]{:S(2)}) async-start(), calls=%async_computation.7 | async-start | bytes 2654208 | tf_op jit(solution)/shard_map/all_gather | solution.py:125
  9.4 219.7 %all-gather.10.cloned.1.call-start = ((), (), s32[]{:S(2)}) async-start(), calls=%async_computation.6 | async-start | bytes 7864320 | tf_op jit(solution)/shard_map/all_gather | solution.py:151
  10.2 10.1 copy-start.58
  11.6 62.2 %copy-start.46 = (f32[768]{0:T(1024)}, f32[768]{0:T(1024)S(1)}, u32[]{:S(2)}) copy-start(f32[768]{0:T(1024)S(1)} %get-tuple-element.248) | copy-start | bytes 9220
  12.9 60.8 %copy-start.60 = (f32[768]{0:T(1024)}, f32[768]{0:T(1024)S(1)}, u32[]{:S(2)}) copy-start(f32[768]{0:T(1024)S(1)} %get-tuple-element.250) | copy-start | bytes 9220
  20.3 53.4 %copy-start.10 = (f32[1024,768]{0,1:T(8,128)}, f32[1024,768]{0,1:T(8,128)S(1)}, u32[]{:S(2)}) copy-start(f32[1024,768]{0,1:T(8,128)S(1)} %get-tuple-element.314) | copy-start | bytes 9437188
  20.3 59.6 %copy-start.38 = (f32[1024]{0:T(1024)}, f32[1024]{0:T(1024)S(1)}, u32[]{:S(2)}) copy-start(f32[1024]{0:T(1024)S(1)} %broadcast_multiply_fusion.1) | copy-start | bytes 12292
  21.6 58.3 %copy-start.48 = (f32[1024]{0:T(1024)}, f32[1024]{0:T(1024)S(1)}, u32[]{:S(2)}) copy-start(f32[1024]{0:T(1024)S(1)} %fusion.47) | copy-start | bytes 12292
  85.1 23.0 %copy-start.9 = (bf16[1024,12,64]{0,2,1:T(8,128)(2,1)S(1)}, bf16[1024,12,64]{0,2,1:T(8,128)(2,1)}, u32[]{:S(2)}) copy-start(bf16[1024,12,64]{0,2,1:T(8,128)(2,1)} %get-tuple-element.479) | copy-start | bytes 4718596 | tf_op jit(solution)/shard_map/while/body/eval_jaxpr/while
  95.7 15.4 %copy-start = (f32[12,512,1024]{2,1,0:T(8,128)S(1)}, f32[12,512,1024]{2,1,0:T(8,128)}, u32[]{:S(2)}) copy-start(f32[12,512,1024]{2,1,0:T(8,128)} %get-tuple-element.433) | copy-start | bytes 75497472 | tf_op jit(solution)/shard_map/while/body/eval_jaxpr/while
  121.4 23.1 %copy-start.9 = (bf16[1024,12,64]{0,2,1:T(8,128)(2,1)S(1)}, bf16[1024,12,64]{0,2,1:T(8,128)(2,1)}, u32[]{:S(2)}) copy-start(bf16[1024,12,64]{0,2,1:T(8,128)(2,1)} %get-tuple-element.479) | copy-start | bytes 4718596 | tf_op jit(solution)/shard_map/while/body/eval_jaxpr/while
  132.1 15.7 %copy-start = (f32[12,512,1024]{2,1,0:T(8,128)S(1)}, f32[12,512,1024]{2,1,0:T(8,128)}, u32[]{:S(2)}) copy-start(f32[12,512,1024]{2,1,0:T(8,128)} %get-tuple-element.433) | copy-start | bytes 75497472 | tf_op jit(solution)/shard_map/while/body/eval_jaxpr/while
  156.3 5.9 copy-start.1
  156.3 5.9 copy-start.4
  156.4 5.9 copy-start.25
  156.4 5.9 copy-start.63
  169.9 107.0 %all-gather.14.cloned.1.call-start = ((), (), s32[]{:S(2)}) async-start(), calls=%async_computation.9 | async-start | bytes 7864320 | tf_op jit(solution)/shard_map/all_gather | solution.py:167
  170.5 189.2 %reduce-scatter.7.cloned.1.call-start = ((), (), s32[]{:S(2)}) async-start(), calls=%async_computation.10 | async-start | bytes 7864320 | tf_op jit(solution)/shard_map/reduce_scatter | solution.py:181
  182.2 94.7 %copy-start.65 = (bf16[2,768,768]{2,1,0:T(8,128)(2,1)S(1)}, bf16[2,768,768]{2,1,0:T(8,128)(2,1)}, u32[]{:S(2)}) copy-start(bf16[2,768,768]{2,1,0:T(8,128)(2,1)} %all-gather.12.cloned.1.call-done) | copy-start | bytes 7077892
  292.1 2.6 copy-start.67
  301.7 3.0 copy-start.51
  301.7 336.9 %reduce-scatter.5.cloned.1.call-start = ((), (), s32[]{:S(2)}) async-start(), calls=%async_computation.8 | async-start | bytes 7864320 | tf_op jit(solution)/shard_map/reduce_scatter | solution.py:158
  315.5 44.3 %copy-start.7 = (f32[1024,768]{0,1:T(8,128)S(1)}, f32[1024,768]{0,1:T(8,128)}, u32[]{:S(2)}) copy-start(f32[1024,768]{0,1:T(8,128)} %copy-done.6) | copy-start | bytes 9437188
  315.5 44.3 %copy-start.28 = (f32[1024]{0:T(1024)S(1)}, f32[1024]{0:T(1024)}, u32[]{:S(2)}) copy-start(f32[1024]{0:T(1024)} %copy-done.27) | copy-start | bytes 12292
  315.5 44.3 %copy-start.32 = (f32[768]{0:T(1024)S(1)}, f32[768]{0:T(1024)}, u32[]{:S(2)}) copy-start(f32[768]{0:T(1024)} %get-tuple-element.247) | copy-start | bytes 9220
  315.5 47.4 %copy-start.45 = (f32[1024]{0:T(1024)S(1)}, f32[1024]{0:T(1024)}, u32[]{:S(2)}) copy-start(f32[1024]{0:T(1024)} %copy-done.44) | copy-start | bytes 12292
  315.5 47.4 %copy-start.36 = (f32[1024]{0:T(1024)S(1)}, f32[1024]{0:T(1024)}, u32[]{:S(2)}) copy-start(f32[1024]{0:T(1024)} %copy-done.35) | copy-start | bytes 12292
  315.5 489.6 %all-reduce.6.cloned.1.call-start = ((), (), s32[]{:S(2)}) async-start(), calls=%async_computation.13 | async-start | bytes 19218432 | tf_op jit(solution)/shard_map/psum | solution.py:241
  359.8 3.1 copy-start.14
  362.9 4.3 copy-start.40
  367.2 2.6 copy-start.22
  367.2 2.6 copy-start.2
  373.9 12.2 %copy-start.19 = (bf16[1024,12,64]{0,2,1:T(8,128)(2,1)S(1)}, bf16[1024,12,64]{0,2,1:T(8,128)(2,1)}, u32[]{:S(2)}) copy-start(bf16[1024,12,64]{0,2,1:T(8,128)(2,1)} %get-tuple-element.525) | copy-start | bytes 4718596 | tf_op jit(solution)/shard_map/while/body/eval_jaxpr/while
  439.0 9.5 copy-start.5
  460.7 11.5 %copy-start.19 = (bf16[1024,12,64]{0,2,1:T(8,128)(2,1)S(1)}, bf16[1024,12,64]{0,2,1:T(8,128)(2,1)}, u32[]{:S(2)}) copy-start(bf16[1024,12,64]{0,2,1:T(8,128)(2,1)} %get-tuple-element.525) | copy-start | bytes 4718596 | tf_op jit(solution)/shard_map/while/body/eval_jaxpr/while
  525.8 9.5 copy-start.5
  549.1 6.6 copy-start.3
  559.7 6.0 copy-start.11
  559.7 6.0 copy-start.39
  559.7 6.0 copy-start.47
  559.7 6.0 copy-start.49
  559.7 6.0 copy-start.61
  599.0 3.0 copy-start.43
  599.0 3.0 copy-start.12
  599.0 3.8 copy-start.13
  602.8 3.5 copy-start.15
  602.8 4.0 copy-start.17
  602.8 4.0 copy-start.29
  602.8 4.0 copy-start.33
  602.8 4.0 copy-start.34
  602.8 3.9 copy-start.37
  602.8 3.9 copy-start.41
  602.8 3.9 copy-start.53
  610.6 294.3 %reduce-scatter.11.cloned.1.call-start = ((), (), s32[]{:S(2)}) async-start(), calls=%async_computation.12 | async-start | bytes 5308416 | tf_op jit(solution)/shard_map/reduce_scatter | solution.py:189
  631.3 4.9 copy-start.62
  631.4 5.5 copy-start.55
  631.4 5.5 copy-start.56
  631.4 5.5 copy-start.57
  631.4 378.4 %reduce-scatter.9.cloned.1.call-start = ((), (), s32[]{:S(2)}) async-start(), calls=%async_computation.11 | async-start | bytes 2433024 | tf_op jit(solution)/shard_map/reduce_scatter | solution.py:239
  644.6 3.7 copy-start.21
  (18 other events, 32.1 us)
Sparse Core Ops, SparseCore 0:
  10.9 62.7 all-gather.5
  76.6 52.6 all-gather.7
  131.6 50.5 all-gather.11
  184.2 44.8 all-gather.9
  230.5 46.3 all-gather.13
  301.8 57.8 reduce-scatter.6
  362.3 57.8 reduce-scatter.4
  610.7 194.4 all-reduce.5
  809.4 95.4 reduce-scatter.10
  910.6 99.1 reduce-scatter.8
where the time goes:
time: 1030 us; the launch traced here: 1020 us
  waiting for transfers between devices  486 us (47%)
  matrix products  292 us (28%)
  other arithmetic  100 us (10%)
  local copies, waits for them, and re-layouts  75.8 us (7%)
  blocking collectives  41.1 us (4%)
  between operations  15.2 us (1%)
    psum x1, waiting for transfers between devices, local(): lax.psum((grad_prompts, jnp.stack([grad_gain_one, grad_gain_two]), jnp.st...  114 us
    reduce_scatter x1, waiting for transfers between devices, local(): lax.psum_scatter(grad_out_weight, ('dp', 'mp'), scatter_dimension=0, tile...  105 us
    reduce_scatter x1, waiting for transfers between devices, local(): mlp_grad = lax.psum_scatter(grad_mlp, 'dp', scatter_dimension=1, tiled=True)  98 us
    all_gather x1, waiting for transfers between devices, local(): lax.all_gather(attn_qkv, ('dp', 'mp'), axis=1, tiled=True)  52.1 us
    all_gather x1, waiting for transfers between devices, local(): gathered = lax.all_gather(normed_two, 'mp', axis=0, tiled=True)  46.9 us
    dot_general x4, matrix products, masked_scores(): jnp.einsum('qhd,khd->hqk', query_tile, key_heads, preferred_element_type=...  44.9 us
    reduce_scatter x1, waiting for transfers between devices, local(): lax.psum_scatter(jnp.einsum('tf,df->td', piece, mlp_part[0], preferred_el...  44.2 us
    convert_element_type x2, other arithmetic, one_tile(): grad_scores = (weights * (grad_weights - weighted)).astype(jnp.bfloat16)  42.6 us
  transfers between devices with their start and end apart: 10, of which 8 were waited for; matrix products, arithmetic and copies ran while one was open for 42% of the time, Pallas kernels for 0%

commit v1 on v0

--- a/solution.py
+++ b/solution.py
@@ -10,6 +10,12 @@
 EPS = 1e-06
 HIGHEST = lax.Precision.HIGHEST
 MASKED = -1e30
+
+
+def laid_out(parts, dim):
+    parts = jnp.moveaxis(parts, 0, dim)
+    lengths = parts.shape
+    return parts.reshape(*lengths[:dim], lengths[dim] * lengths[dim + 1], *lengths[dim + 2 :])
 
 
 def layer_norm(value_list, gain_row, shift_row):
@@ -148,7 +154,14 @@
     normed_two = layer_norm(middle, norm_gain[1], norm_shift[1]).astype(jnp.bfloat16)
     grad_output = cotangent.astype(jnp.float32)
     grad_down = jnp.sum(grad_output, axis=0)
-    gathered = lax.all_gather(normed_two, "mp", axis=0, tiled=True)
+    size = lax.axis_size("mp")
+    ahead = [(i, (i + 1) % size) for i in range(size)]
+    tiles = [normed_two]
+    while len(tiles) < size:
+        tiles.append(lax.ppermute(tiles[-1], "mp", ahead))
+    index = lax.axis_index("mp")
+    tiles = jnp.stack(tiles)[(index - jnp.arange(size)) % size]
+    gathered = laid_out(tiles, 0)
     unit_count = mlp_part.shape[2]
     offset = lax.axis_index("mp") * unit_count
     bias_part = lax.dynamic_slice_in_dim(mlp_bias_up, offset, unit_count, 0)

time: 1030 us -> 906 us (0.88)
  waiting for transfers between devices: 486 us -> 342 us
  local copies, waits for them, and re-layouts: 75.8 us -> 89.9 us
    reduce_scatter x1, waiting for transfers between devices: 98 us -> 0.01 us  [local(): mlp_grad = lax.psum_scatter(grad_mlp, 'dp', scatter_dimension=1, tiled=True)]
    reduce_scatter x1, waiting for transfers between devices: 105 us -> 31.4 us  [local(): lax.psum_scatter(grad_out_weight, ('dp', 'mp'), scatter_dimension=0, tile...]
    ppermute x0 -> x3, waiting for transfers between devices: none -> 58.8 us  [local(): tiles.append(lax.ppermute(tiles[-1], 'mp', ahead))]
    all_gather x1 -> x0, waiting for transfers between devices: 46.9 us -> none  [local(): gathered = lax.all_gather(normed_two, 'mp', axis=0, tiled=True)]
    psum x1, waiting for transfers between devices: 114 us -> 155 us  [local(): lax.psum((grad_prompts, jnp.stack([grad_gain_one, grad_gain_two]), jnp.st...]
    gather x0 -> x2, local copies, waits for them, and re-layouts: none -> 15.1 us  [local(): tiles = jnp.stack(tiles)[(index - jnp.arange(size)) % size]]
    all_gather x1, waiting for transfers between devices: 12.4 us -> 0.01 us  [local(): grad_gathered = lax.all_gather(cotangent, 'mp', axis=0, tiled=True)]
    all_gather x1, waiting for transfers between devices: 10.8 us -> 0.01 us  [local(): mlp_part = lax.all_gather(mlp_weight, 'dp', axis=1, tiled=True)]
  transfers between devices with their start and end apart: 10 -> 12, of which waited for: 8 -> 7; matrix products, arithmetic and copies ran while one was open for 42% -> 49% of each run, Pallas kernels for 0% -> 0%
where the time goes in v1:
time: 906 us; the launch traced here: 898 us
  waiting for transfers between devices  342 us (38%)
  matrix products  291 us (32%)
  other arithmetic  107 us (12%)
  local copies, waits for them, and re-layouts  89.9 us (10%)
  blocking collectives  43.2 us (5%)
  between operations  16.3 us (2%)
    psum x1, waiting for transfers between devices, local(): lax.psum((grad_prompts, jnp.stack([grad_gain_one, grad_gain_two]), jnp.st...  155 us
    ppermute x3, waiting for transfers between devices, local(): tiles.append(lax.ppermute(tiles[-1], 'mp', ahead))  58.8 us
    all_gather x1, waiting for transfers between devices, local(): lax.all_gather(attn_qkv, ('dp', 'mp'), axis=1, tiled=True)  52.8 us
    dot_general x4, matrix products, masked_scores(): jnp.einsum('qhd,khd->hqk', query_tile, key_heads, preferred_element_type=...  45 us
    psum x1, blocking collectives, local(): lax.psum((grad_prompts, jnp.stack([grad_gain_one, grad_gain_two]), jnp.st...  43.2 us
    reduce_scatter x1, waiting for transfers between devices, local(): lax.psum_scatter(jnp.einsum('tf,df->td', piece, mlp_part[0], preferred_el...  42.9 us
    convert_element_type x2, other arithmetic, one_tile(): grad_scores = (weights * (grad_weights - weighted)).astype(jnp.bfloat16)  42.6 us
    dot_general x2, matrix products, one_tile(): jnp.einsum('qhd,khd->hqk', grad_tile, value_heads, preferred_element_type...  36.4 us
  transfers between devices with their start and end apart: 12, of which 7 were waited for; matrix products, arithmetic and copies ran while one was open for 49% of the time, Pallas kernels for 0%

profile of v1, /device:TPU:0, one launch (start us, length us, event | category | flops | bytes accessed | tf_op | source)
XLA Modules:
  0.0 898.0 jit_solution(10787307791852259950)
XLA Ops:
  14.6 2.6 copy.59
  17.2 3.2 fusion.61
  21.7 52.8 %all-gather.5.cloned.1.call-done = bf16[3,768,768]{2,1,0:T(8,128)(2,1)} async-done(((bf16[3,24,768]{2,1,0:T(8,128)(2,1)}), bf16[3,768,768]{2,1,0:T(8,128)(2,1)}) %all-gather.5.cloned.1.call-update) | async-done | bytes 3538960 | tf_op jit(solution)/shard_map/all_gather | solution.py:128
  74.6 6.2 convolution_bitcast_fusion
  83.7 72.8 %while.47 = (s32[]{:T(128)}, bf16[2,512,12,64]{1,3,2,0:T(8,128)(2,1)}, f32[2,12,512]{2,1,0:T(8,128)S(1)}, s32[2]{0:T(128)S(1)}, s32[1024]{0:T(1024)S(1)}, /*inde...) while((s32[]{:T(128)}, ...), condition=%wide.region_5.6_spmd, body=%wide.region_2.5_spmd.sunk | while | flops 1687021568 | bytes 189499632 | solution.py:57
  85.6 10.6 %fusion.106 = (f32[12,512]{1,0:T(8,128)S(1)}, f32[12,512,1024]{2,1,0:T(8,128)}) fusion(pred[512,1024]{1,0:T(8,128)(4,1)S(1)} %broadcast_compare_fusion.5, bf16[1024,12,64]{0,2,1:T(8,128)(2,1)S(1)} %get-tuple-element.478, bf16[1024,12,64]{0,2,1:T(8,128)(2,1)S(1)} %get-tuple-element.477, s32[]{:T(128)S(6)} %select_n.111), kind=kOutput, calls=%fused_computation.4.clone.1 | convolution fusion | flops 824174592 | bytes 28073988 | tf_op jit(solution)/shard_map/while/body/eval_jaxpr/while/body/eval_jaxpr/qhd,khd->hqk/dot_general | solution.py:34
  96.2 12.3 %fusion.107 = f32[12,512]{1,0:T(8,128)S(1)} fusion(f32[12,512,1024]{2,1,0:T(8,128)} %get-tuple-element.433, f32[12,512]{1,0:T(8,128)S(1)} %get-tuple-element.434, pred[512,1024]{1,0:T(8,128)(4,1)S(1)} %broadcast_compare_fusion.5), kind=kLoop, calls=%fused_computation.5.clone.1 | loop fusion | flops 25159680 | bytes 25739264 | tf_op jit(solution)/shard_map/while/body/eval_jaxpr/while/body/eval_jaxpr/reduce_sum | solution.py:52
  108.6 3.1 copy-done
  111.6 8.5 fusion.108
  121.9 10.7 %fusion.106 = (f32[12,512]{1,0:T(8,128)S(1)}, f32[12,512,1024]{2,1,0:T(8,128)}) fusion(pred[512,1024]{1,0:T(8,128)(4,1)S(1)} %broadcast_compare_fusion.5, bf16[1024,12,64]{0,2,1:T(8,128)(2,1)S(1)} %get-tuple-element.478, bf16[1024,12,64]{0,2,1:T(8,128)(2,1)S(1)} %get-tuple-element.477, s32[]{:T(128)S(6)} %select_n.111), kind=kOutput, calls=%fused_computation.4.clone.1 | convolution fusion | flops 824174592 | bytes 28073988 | tf_op jit(solution)/shard_map/while/body/eval_jaxpr/while/body/eval_jaxpr/qhd,khd->hqk/dot_general | solution.py:34
  132.6 12.3 %fusion.107 = f32[12,512]{1,0:T(8,128)S(1)} fusion(f32[12,512,1024]{2,1,0:T(8,128)} %get-tuple-element.433, f32[12,512]{1,0:T(8,128)S(1)} %get-tuple-element.434, pred[512,1024]{1,0:T(8,128)(4,1)S(1)} %broadcast_compare_fusion.5), kind=kLoop, calls=%fused_computation.5.clone.1 | loop fusion | flops 25159680 | bytes 25739264 | tf_op jit(solution)/shard_map/while/body/eval_jaxpr/while/body/eval_jaxpr/reduce_sum | solution.py:52
  144.9 3.1 copy-done
  148.0 8.5 fusion.108
  156.5 4.2 copy.61
  162.4 4.2 fusion.62
  169.6 19.9 %collective-permute-done = bf16[1024,768]{0,1:T(8,128)(2,1)} collective-permute-done((bf16[1024,768]{0,1:T(8,128)(2,1)}, bf16[1024,768]{0,1:T(8,128)(2,1)}, u32[]{:S(2)}, u32[]{:S(2)}) %collective-permute-start) | collective-permute-done | bytes 1572896 | tf_op jit(solution)/shard_map/ppermute | solution.py:161
  189.5 20.2 %collective-permute-done.1 = bf16[1024,768]{0,1:T(8,128)(2,1)} collective-permute-done((bf16[1024,768]{0,1:T(8,128)(2,1)}, bf16[1024,768]{0,1:T(8,128)(2,1)}, u32[]{:S(2)}, u32[]{:S(2)}) %collective-permute-start.1) | collective-permute-done | bytes 1572896 | tf_op jit(solution)/shard_map/ppermute | solution.py:161
  211.0 18.7 %collective-permute-done.2 = bf16[1024,768]{0,1:T(8,128)(2,1)} collective-permute-done((bf16[1024,768]{0,1:T(8,128)(2,1)}, bf16[1024,768]{0,1:T(8,128)(2,1)}, u32[]{:S(2)}, u32[]{:S(2)}) %collective-permute-start.2) | collective-permute-done | bytes 1572896 | tf_op jit(solution)/shard_map/ppermute | solution.py:161
  229.8 6.7 pad_maximum_fusion
  236.4 6.4 gather_fusion
  242.8 8.7 copy.62
  251.6 34.7 %multiply_convert_fusion.1 = (bf16[4096,768]{1,0:T(8,128)(2,1)}, f32[4096,768]{1,0:T(8,128)}, f32[4096,768]{1,0:T(8,128)}) fusion(f32[768]{0:T(1024)S(1)} %dynamic_slice.51, bf16[4096,768]{1,0:T(8,128)(2,1)} %bitcast.130, bf16[2,768,768]{2,1,0:T(8,128)(2,1)} %all-gather.9.cloned.1.call-done), kind=kOutput, calls=%fused_computation.44 | convolution fusion | flops 5039456256 | bytes 38931456 | tf_op jit(solution)/shard_map/dot_general | solution.py:168
  286.3 15.2 %convert_reduce_fusion = (f32[768]{0:T(1024)}, bf16[4096,768]{1,0:T(8,128)(2,1)S(1)}) fusion(f32[4096,768]{1,0:T(8,128)} %get-tuple-element.303, bf16[4096,768]{1,0:T(8,128)(2,1)} %all-gather.11.cloned.1.call-done, bf16[2,768,768]{2,1,0:T(8,128)(2,1)S(1)} %copy-done.65, f32[4096,768]{1,0:T(8,128)} %get-tuple-element.317, f32[768]{0:T(1024)S(1)} %dynamic_slice.51), kind=kOutput, calls=%fused_computation.42 | convolution fusion | flops 4885314560 | bytes 38935552 | tf_op jit(solution)/shard_map/dot_general | solution.py:181
  301.5 2.6 copy-done.67
  304.1 7.0 convolution_convert_fusion
  315.0 9.6 %convolution_convert_fusion.1 = bf16[4096,768]{0,1:T(8,128)(2,1)} fusion(bf16[4096,768]{1,0:T(8,128)(2,1)} %get-tuple-element.302, bf16[2,768,768]{2,1,0:T(8,128)(2,1)} %all-gather.9.cloned.1.call-done), kind=kOutput, calls=%fused_computation.59 | convolution fusion | flops 4834983936 | bytes 13762560 | tf_op jit(solution)/shard_map/tf,df->td/dot_general | solution.py:172
  324.7 42.9 %reduce-scatter.7.cloned.1.call-done = bf16[1024,768]{0,1:T(8,128)(2,1)} async-done(((bf16[4096,768]{0,1:T(8,128)(2,1)}), bf16[1024,768]{0,1:T(8,128)(2,1)}) %reduce-scatter.7.cloned.1.call-update) | async-done | bytes 1572880 | tf_op jit(solution)/shard_map/reduce_scatter | solution.py:194
  367.6 3.1 convert_reduce_fusion.1
  370.8 2.2 fusion.38
  375.1 2.6 convolution_convert_fusion.2
  377.7 175.1 %while.48 = (s32[]{:T(128)}, f32[1024,12,64]{0,2,1:T(8,128)}, f32[1024,12,64]{0,2,1:T(8,128)}, bf16[2,512,12,64]{1,3,2,0:T(8,128)(2,1)}, s32[2]{0:T(128)S(1)}, /...) while((s32[]{:T(128)}, f32[1024,12,64]{0,2,1:T(8,128)}, ...), condition=%wide.region_14.15_spmd.clone, body=%wide.region_12.14_spmd.clone.sunk | while | flops 4125747200 | bytes 225634640 | solution.py:98
  381.5 12.2 %fusion.118 = f32[12,512,1024]{2,1,0:T(8,128)} fusion(bf16[1024,12,64]{0,2,1:T(8,128)(2,1)S(1)} %get-tuple-element.523, bf16[1024,12,64]{0,2,1:T(8,128)(2,1)} %get-tuple-element.521, s32[]{:T(128)S(6)} %select_n.115), kind=kOutput, calls=%fused_computation.31.clone.1 | convolution fusion | flops 805306368 | bytes 27525124 | tf_op jit(solution)/shard_map/while/body/eval_jaxpr/while/body/eval_jaxpr/qhd,khd->hqk/dot_general | solution.py:34
  393.7 13.3 %bitcast_add_fusion.5 = f32[1024,12,64]{0,2,1:T(8,128)} fusion(f32[1024,12,64]{0,2,1:T(8,128)} %get-tuple-element.502, f32[12,512,1024]{2,1,0:T(8,128)} %fusion.118, f32[12,512]{1,0:T(8,128)S(1)} %dynamic-slice_bitcast_fusion.2, pred[512,1024]{1,0:T(8,128)(4,1)S(1)} %broadcast_compare_fusion.6, pred[]{:T(512)S(6)} %compare.11, ...), kind=kOutput, calls=%fused_computation.23.clone.1 | convolution fusion | flops 832045056 | bytes 32800772 | tf_op jit(solution)/shard_map/while/body/eval_jaxpr/while/body/eval_jaxpr/hqk,qhd->khd/dot_general | solution.py:89
  407.0 18.3 %multiply_reduce_fusion.6 = (f32[12,512]{1,0:T(8,128)S(1)}, f32[12,512,1024]{2,1,0:T(8,128)}) fusion(f32[12,512,1024]{2,1,0:T(8,128)} %fusion.118, f32[12,512]{1,0:T(8,128)S(1)} %dynamic-slice_bitcast_fusion.2, pred[512,1024]{1,0:T(8,128)(4,1)S(1)} %broadcast_compare_fusion.6, bf16[1024,12,64]{0,2,1:T(8,128)(2,1)} %get-tuple-element.526, ...), kind=kOutput, calls=%fused_computation.18.clone.1 | convolution fusion | flops 836757504 | bytes 53264388 | tf_op jit(solution)/shard_map/while/body/eval_jaxpr/while/body/eval_jaxpr/qhd,khd->hqk/dot_general | solution.py:73
  425.3 21.4 %multiply_convert_fusion.3 = bf16[12,512,1024]{2,1,0:T(8,128)(2,1)} fusion(f32[12,512,1024]{2,1,0:T(8,128)} %get-tuple-element.446, f32[12,512,1024]{2,1,0:T(8,128)} %fusion.118, f32[12,512]{1,0:T(8,128)S(1)} %get-tuple-element.447, f32[12,512]{1,0:T(8,128)S(1)} %dynamic-slice_bitcast_fusion.2, pred[512,1024]{1,0:T(8,128)(4,1)S(1)} %broadcast_compare_fusion.6), kind=kLoop, calls=%fused_computation.17.clone.1 | loop fusion | flops 37748736 | bytes 63488000 | tf_op jit(solution)/shard_map/while/body/eval_jaxpr/while/body/eval_jaxpr/convert_element_type | solution.py:77
  446.7 9.5 %bitcast_dynamic-update-slice_fusion.5 = bf16[2,512,12,64]{1,3,2,0:T(8,128)(2,1)} fusion(bf16[2,512,12,64]{1,3,2,0:T(8,128)(2,1)} %get-tuple-element.503, s32[]{:T(128)S(6)} %copy.104, bf16[12,512,1024]{2,1,0:T(8,128)(2,1)} %multiply_convert_fusion.3, bf16[1024,12,64]{0,2,1:T(8,128)(2,1)S(1)} %get-tuple-element.523), kind=kOutput, calls=%fused_computation.25.clone.1 | convolution fusion | flops 805699584 | bytes 15728644 | tf_op jit(solution)/shard_map/while/body/eval_jaxpr/while/body/eval_jaxpr/hqk,khd->qhd/dot_general | solution.py:79
  456.2 8.6 bitcast_add_fusion.4
  468.4 11.5 %fusion.118 = f32[12,512,1024]{2,1,0:T(8,128)} fusion(bf16[1024,12,64]{0,2,1:T(8,128)(2,1)S(1)} %get-tuple-element.523, bf16[1024,12,64]{0,2,1:T(8,128)(2,1)} %get-tuple-element.521, s32[]{:T(128)S(6)} %select_n.115), kind=kOutput, calls=%fused_computation.31.clone.1 | convolution fusion | flops 805306368 | bytes 27525124 | tf_op jit(solution)/shard_map/while/body/eval_jaxpr/while/body/eval_jaxpr/qhd,khd->hqk/dot_general | solution.py:34
  479.8 14.2 %bitcast_add_fusion.5 = f32[1024,12,64]{0,2,1:T(8,128)} fusion(f32[1024,12,64]{0,2,1:T(8,128)} %get-tuple-element.502, f32[12,512,1024]{2,1,0:T(8,128)} %fusion.118, f32[12,512]{1,0:T(8,128)S(1)} %dynamic-slice_bitcast_fusion.2, pred[512,1024]{1,0:T(8,128)(4,1)S(1)} %broadcast_compare_fusion.6, pred[]{:T(512)S(6)} %compare.11, ...), kind=kOutput, calls=%fused_computation.23.clone.1 | convolution fusion | flops 832045056 | bytes 32800772 | tf_op jit(solution)/shard_map/while/body/eval_jaxpr/while/body/eval_jaxpr/hqk,qhd->khd/dot_general | solution.py:89
  494.0 18.1 %multiply_reduce_fusion.6 = (f32[12,512]{1,0:T(8,128)S(1)}, f32[12,512,1024]{2,1,0:T(8,128)}) fusion(f32[12,512,1024]{2,1,0:T(8,128)} %fusion.118, f32[12,512]{1,0:T(8,128)S(1)} %dynamic-slice_bitcast_fusion.2, pred[512,1024]{1,0:T(8,128)(4,1)S(1)} %broadcast_compare_fusion.6, bf16[1024,12,64]{0,2,1:T(8,128)(2,1)} %get-tuple-element.526, ...), kind=kOutput, calls=%fused_computation.18.clone.1 | convolution fusion | flops 836757504 | bytes 53264388 | tf_op jit(solution)/shard_map/while/body/eval_jaxpr/while/body/eval_jaxpr/qhd,khd->hqk/dot_general | solution.py:73
  512.2 21.2 %multiply_convert_fusion.3 = bf16[12,512,1024]{2,1,0:T(8,128)(2,1)} fusion(f32[12,512,1024]{2,1,0:T(8,128)} %get-tuple-element.446, f32[12,512,1024]{2,1,0:T(8,128)} %fusion.118, f32[12,512]{1,0:T(8,128)S(1)} %get-tuple-element.447, f32[12,512]{1,0:T(8,128)S(1)} %dynamic-slice_bitcast_fusion.2, pred[512,1024]{1,0:T(8,128)(4,1)S(1)} %broadcast_compare_fusion.6), kind=kLoop, calls=%fused_computation.17.clone.1 | loop fusion | flops 37748736 | bytes 63488000 | tf_op jit(solution)/shard_map/while/body/eval_jaxpr/while/body/eval_jaxpr/convert_element_type | solution.py:77
  533.4 9.5 %bitcast_dynamic-update-slice_fusion.5 = bf16[2,512,12,64]{1,3,2,0:T(8,128)(2,1)} fusion(bf16[2,512,12,64]{1,3,2,0:T(8,128)(2,1)} %get-tuple-element.503, s32[]{:T(128)S(6)} %copy.104, bf16[12,512,1024]{2,1,0:T(8,128)(2,1)} %multiply_convert_fusion.3, bf16[1024,12,64]{0,2,1:T(8,128)(2,1)S(1)} %get-tuple-element.523), kind=kOutput, calls=%fused_computation.25.clone.1 | convolution fusion | flops 805699584 | bytes 15728644 | tf_op jit(solution)/shard_map/while/body/eval_jaxpr/while/body/eval_jaxpr/hqk,khd->qhd/dot_general | solution.py:79
  542.9 9.5 %bitcast_add_fusion.4 = f32[1024,12,64]{0,2,1:T(8,128)} fusion(f32[1024,12,64]{0,2,1:T(8,128)} %get-tuple-element.501, bf16[12,512,1024]{2,1,0:T(8,128)(2,1)} %multiply_convert_fusion.3, pred[]{:T(512)S(6)} %compare.11, bf16[1024,12,64]{0,2,1:T(8,128)(2,1)S(1)} %copy-done.8, s32[]{:T(128)S(6)} %select_n.115), kind=kOutput, calls=%fused_computation.24.clone.1 | convolution fusion | flops 807665664 | bytes 19660804 | tf_op jit(solution)/shard_map/while/body/eval_jaxpr/while/body/eval_jaxpr/hqk,qhd->khd/dot_general | solution.py:84
  552.8 4.2 copy.66
  557.0 4.0 stack_reshape.12
  561.0 2.6 copy.67
  564.9 2.6 copy.68
  567.6 3.4 convert_reduce_fusion.4
  570.9 2.6 copy.69
  573.6 9.4 %convolution_bitcast_fusion.1 = f32[3,768,768]{1,2,0:T(8,128)} fusion(bf16[1,1024,768]{2,1,0:T(8,128)(2,1)} %copy.69, bf16[1,1024,768]{2,1,0:T(8,128)(2,1)} %copy.68, bf16[1,1024,768]{2,1,0:T(8,128)(2,1)} %copy.67, f32[1024,768]{0,1:T(8,128)S(1)} %copy-done.11, f32[768]{0:T(1024)S(1)} %copy-done.61, f32[768]{0:T(1024)S(1)} %copy-done.48, ...), kind=kOutput, calls=%fused_computation.91 | convolution fusion | flops 3632529408 | bytes 14956544 | tf_op jit(solution)/shard_map/td,cte->cde/dot_general | solution.py:232
  583.0 11.0 %copy.74 = f32[3,768,768]{2,0,1:T(4,128)} copy(f32[3,768,768]{1,2,0:T(8,128)} %convolution_bitcast_fusion.1) | data formatting | bytes 14155776 | tf_op jit(solution)/shard_map/td,cte->cde/transpose | solution.py:232
  594.0 9.0 fusion.63
  602.9 3.9 copy.70
  606.8 3.0 multiply_reduce_fusion.1
  614.6 3.8 fusion.45
  618.4 9.3 %convolution_bitcast_fusion.3 = f32[1,768,768]{2,1,0:T(8,128)S(1)} fusion(bf16[4096,768]{1,0:T(8,128)(2,1)} %bitcast.131, bf16[4096,768]{1,0:T(8,128)(2,1)} %copy-done.67), kind=kOutput, calls=%fused_computation.97 | convolution fusion | flops 4831838208 | bytes 14942208 | tf_op jit(solution)/shard_map/td,tf->df/dot_general | solution.py:186
  627.8 9.2 %convolution_bitcast_fusion.2 = f32[1,768,768]{2,1,0:T(8,128)S(1)} fusion(bf16[4096,768]{1,0:T(8,128)(2,1)} %get-tuple-element.302, bf16[4096,768]{1,0:T(8,128)(2,1)} %all-gather.11.cloned.1.call-done), kind=kOutput, calls=%fused_computation.96 | convolution fusion | flops 4831838208 | bytes 14942208 | tf_op jit(solution)/shard_map/td,tf->df/dot_general | solution.py:187
  637.0 2.5 pad_maximum_fusion.2
  639.6 4.8 fusion.64
  646.9 5.9 broadcast_select_fusion
  652.8 3.7 copy.77
  658.1 43.2 %all-reduce.2 = (f32[2,768]{1,0:T(2,128)}, f32[2,768]{1,0:T(2,128)}, f32[3,768]{1,0:T(4,128)}, f32[3072]{0:T(1024)}, f32[768]{0:T(1024)}) all-reduce(f32[2,768]{1,0:T(2,128)S(1)} %pad_maximum_fusion.8, f32[2,768]{1,0:T(2,128)S(1)} %pad_maximum_fusion.9, ...), channel_id=1, replica_groups=mesh['dp'=8,'mp'=4] {'dp','mp'}, use_global_device_ids=true, to_apply=%region_20.21 | all-reduce | flops 9216 | bytes 73728 | tf_op jit(solution)/shard_map/psum | solution.py:254
  701.3 154.5 %all-reduce.6.cloned.1.call-done = (f32[50,768]{1,0:T(8,128)}, f32[3,768,768]{2,0,1:T(4,128)}) async-done(((f32[50,768]{1,0:T(8,128)}, f32[3,768,768]{2,0,1:T(4,128)}), (f32[50,768]{1,0:T(8,128)}, f32[3,768,768]{2,0,1:T(4,128)})) %all-reduce.6.cloned.1.call-update) | async-done | bytes 7231504 | tf_op jit(solution)/shard_map/psum | solution.py:254
  857.6 31.4 %reduce-scatter.9.cloned.1.call-done = f32[24,768]{1,0:T(8,128)} async-done(((f32[768,768]{1,0:T(8,128)}), f32[24,768]{1,0:T(8,128)}) %reduce-scatter.9.cloned.1.call-update) | async-done | bytes 73744 | tf_op jit(solution)/shard_map/reduce_scatter | solution.py:252
  (237 shorter events, 40.4 us)
Async XLA Ops:
  8.0 9.2 %copy-start.51 = (s32[1024]{0:T(1024)S(1)}, s32[1024]{0:T(1024)}, u32[]{:S(2)}) copy-start(s32[1024]{0:T(1024)} %param.21) | copy-start | bytes 12292
  8.0 9.2 %copy-start.33 = (f32[50,768]{1,0:T(8,128)S(1)}, f32[50,768]{1,0:T(8,128)}, u32[]{:S(2)}) copy-start(f32[50,768]{1,0:T(8,128)} %param.19) | copy-start | bytes 460804
  8.0 66.5 %all-gather.5.cloned.1.call-start = ((), (), s32[]{:S(2)}) async-start(), calls=%async_computation.4 | async-start | bytes 3649536 | tf_op jit(solution)/shard_map/all_gather | solution.py:128
  8.8 153.6 %all-gather.7.cloned.1.call-start = ((), (), s32[]{:S(2)}) async-start(), calls=%async_computation.5 | async-start | bytes 1216512 | tf_op jit(solution)/shard_map/all_gather | solution.py:129
  9.5 242.0 %all-gather.9.cloned.1.call-start = ((), (), s32[]{:S(2)}) async-start(), calls=%async_computation.6 | async-start | bytes 2654208 | tf_op jit(solution)/shard_map/all_gather | solution.py:131
  10.3 10.1 %copy-start.58 = (pred[1024]{0:T(1024)(128)(4,1)}, pred[1024]{0:T(1024)(128)(4,1)S(1)}, u32[]{:S(2)}) copy-start(pred[1024]{0:T(1024)(128)(4,1)S(1)} %broadcast_compare_fusion.2) | copy-start | bytes 3076
  11.7 62.9 %copy-start.47 = (f32[768]{0:T(1024)}, f32[768]{0:T(1024)S(1)}, u32[]{:S(2)}) copy-start(f32[768]{0:T(1024)S(1)} %get-tuple-element.248) | copy-start | bytes 9220
  13.0 61.5 %copy-start.60 = (f32[768]{0:T(1024)}, f32[768]{0:T(1024)S(1)}, u32[]{:S(2)}) copy-start(f32[768]{0:T(1024)S(1)} %get-tuple-element.250) | copy-start | bytes 9220
  20.4 54.2 %copy-start.10 = (f32[1024,768]{0,1:T(8,128)}, f32[1024,768]{0,1:T(8,128)S(1)}, u32[]{:S(2)}) copy-start(f32[1024,768]{0,1:T(8,128)S(1)} %get-tuple-element.314) | copy-start | bytes 9437188
  20.4 60.4 %copy-start.38 = (f32[1024]{0:T(1024)}, f32[1024]{0:T(1024)S(1)}, u32[]{:S(2)}) copy-start(f32[1024]{0:T(1024)S(1)} %broadcast_multiply_fusion.1) | copy-start | bytes 12292
  21.7 59.0 %copy-start.49 = (f32[1024]{0:T(1024)}, f32[1024]{0:T(1024)S(1)}, u32[]{:S(2)}) copy-start(f32[1024]{0:T(1024)S(1)} %fusion.47) | copy-start | bytes 12292
  85.6 23.0 %copy-start.9 = (bf16[1024,12,64]{0,2,1:T(8,128)(2,1)S(1)}, bf16[1024,12,64]{0,2,1:T(8,128)(2,1)}, u32[]{:S(2)}) copy-start(bf16[1024,12,64]{0,2,1:T(8,128)(2,1)} %get-tuple-element.479) | copy-start | bytes 4718596 | tf_op jit(solution)/shard_map/while/body/eval_jaxpr/while
  96.2 15.4 %copy-start = (f32[12,512,1024]{2,1,0:T(8,128)S(1)}, f32[12,512,1024]{2,1,0:T(8,128)}, u32[]{:S(2)}) copy-start(f32[12,512,1024]{2,1,0:T(8,128)} %get-tuple-element.433) | copy-start | bytes 75497472 | tf_op jit(solution)/shard_map/while/body/eval_jaxpr/while
  121.9 23.0 %copy-start.9 = (bf16[1024,12,64]{0,2,1:T(8,128)(2,1)S(1)}, bf16[1024,12,64]{0,2,1:T(8,128)(2,1)}, u32[]{:S(2)}) copy-start(bf16[1024,12,64]{0,2,1:T(8,128)(2,1)} %get-tuple-element.479) | copy-start | bytes 4718596 | tf_op jit(solution)/shard_map/while/body/eval_jaxpr/while
  132.6 15.4 %copy-start = (f32[12,512,1024]{2,1,0:T(8,128)S(1)}, f32[12,512,1024]{2,1,0:T(8,128)}, u32[]{:S(2)}) copy-start(f32[12,512,1024]{2,1,0:T(8,128)} %get-tuple-element.433) | copy-start | bytes 75497472 | tf_op jit(solution)/shard_map/while/body/eval_jaxpr/while
  156.5 5.8 copy-start.1
  156.5 5.8 copy-start.7
  156.5 5.8 copy-start.25
  156.5 5.8 copy-start.63
  166.6 43.9 %copy-start.4 = (f32[1024,768]{0,1:T(8,128)}, f32[1024,768]{0,1:T(8,128)S(1)}, u32[]{:S(2)}) copy-start(f32[1024,768]{0,1:T(8,128)S(1)} %get-tuple-element.316) | copy-start | bytes 9437188
  166.6 43.9 %copy-start.27 = (f32[1024]{0:T(1024)}, f32[1024]{0:T(1024)S(1)}, u32[]{:S(2)}) copy-start(f32[1024]{0:T(1024)S(1)} %broadcast_multiply_fusion) | copy-start | bytes 12292
  167.6 42.9 %copy-start.34 = (f32[1024]{0:T(1024)}, f32[1024]{0:T(1024)S(1)}, u32[]{:S(2)}) copy-start(f32[1024]{0:T(1024)S(1)} %fusion.48) | copy-start | bytes 12292
  169.3 20.2 %collective-permute-start = (bf16[1024,768]{0,1:T(8,128)(2,1)}, bf16[1024,768]{0,1:T(8,128)(2,1)}, u32[]{:S(2)}, u32[]{:S(2)}) collective-permute-start(bf16[1024,768]{0,1:T(8,128)(2,1)} %add_convert_fusion.2), channel_id=1, source_target_pairs={{0,1},{1,2},{2,3},{3,0},{4,5},{5,6},{6,7},{7,4},{8,9},{9,10},{10,1... | collective-permute-start | bytes 4718600 | tf_op jit(solution)/shard_map/ppermute | solution.py:161
  169.5 116.7 %all-gather.11.cloned.1.call-start = ((), (), s32[]{:S(2)}) async-start(), calls=%async_computation.8 | async-start | bytes 7864320 | tf_op jit(solution)/shard_map/all_gather | solution.py:180
  189.5 20.2 %collective-permute-start.1 = (bf16[1024,768]{0,1:T(8,128)(2,1)}, bf16[1024,768]{0,1:T(8,128)(2,1)}, u32[]{:S(2)}, u32[]{:S(2)}) collective-permute-start(bf16[1024,768]{0,1:T(8,128)(2,1)} %collective-permute-done), channel_id=1, source_target_pairs={{0,1},{1,2},{2,3},{3,0},{4,5},{5,6},{6,7},{7,4},{8,9},{9,10},{10,1... | collective-permute-start | bytes 4718600 | tf_op jit(solution)/shard_map/ppermute | solution.py:161
  209.6 20.2 %collective-permute-start.2 = (bf16[1024,768]{0,1:T(8,128)(2,1)}, bf16[1024,768]{0,1:T(8,128)(2,1)}, u32[]{:S(2)}, u32[]{:S(2)}) collective-permute-start(bf16[1024,768]{0,1:T(8,128)(2,1)} %collective-permute-done.1), channel_id=1, source_target_pairs={{0,1},{1,2},{2,3},{3,0},{4,5},{5,6},{6,7},{7,4},{8,9},{9,10},{10,1... | collective-permute-start | bytes 4718600 | tf_op jit(solution)/shard_map/ppermute | solution.py:161
  209.6 158.0 %reduce-scatter.7.cloned.1.call-start = ((), (), s32[]{:S(2)}) async-start(), calls=%async_computation.9 | async-start | bytes 7864320 | tf_op jit(solution)/shard_map/reduce_scatter | solution.py:194
  251.6 34.7 %copy-start.65 = (bf16[2,768,768]{2,1,0:T(8,128)(2,1)S(1)}, bf16[2,768,768]{2,1,0:T(8,128)(2,1)}, u32[]{:S(2)}) copy-start(bf16[2,768,768]{2,1,0:T(8,128)(2,1)} %all-gather.9.cloned.1.call-done) | copy-start | bytes 7077892
  311.1 335.8 %reduce-scatter.5.cloned.1.call-start = ((), (), s32[]{:S(2)}) async-start(), calls=%async_computation.7 | async-start | bytes 7864320 | tf_op jit(solution)/shard_map/reduce_scatter | solution.py:171
  324.6 43.1 %copy-start.5 = (f32[1024,768]{0,1:T(8,128)S(1)}, f32[1024,768]{0,1:T(8,128)}, u32[]{:S(2)}) copy-start(f32[1024,768]{0,1:T(8,128)} %copy-done.4) | copy-start | bytes 9437188
  324.6 43.1 %copy-start.28 = (f32[1024]{0:T(1024)S(1)}, f32[1024]{0:T(1024)}, u32[]{:S(2)}) copy-start(f32[1024]{0:T(1024)} %copy-done.27) | copy-start | bytes 12292
  324.6 43.1 %copy-start.31 = (f32[768]{0:T(1024)S(1)}, f32[768]{0:T(1024)}, u32[]{:S(2)}) copy-start(f32[768]{0:T(1024)} %get-tuple-element.247) | copy-start | bytes 9220
  324.6 46.1 %copy-start.46 = (f32[1024]{0:T(1024)S(1)}, f32[1024]{0:T(1024)}, u32[]{:S(2)}) copy-start(f32[1024]{0:T(1024)} %copy-done.45) | copy-start | bytes 12292
  324.6 46.1 %copy-start.35 = (f32[1024]{0:T(1024)S(1)}, f32[1024]{0:T(1024)}, u32[]{:S(2)}) copy-start(f32[1024]{0:T(1024)} %copy-done.34) | copy-start | bytes 12292
  324.6 531.2 %all-reduce.6.cloned.1.call-start = ((), (), s32[]{:S(2)}) async-start(), calls=%async_computation.12 | async-start | bytes 19218432 | tf_op jit(solution)/shard_map/psum | solution.py:254
  367.6 3.1 copy-start.14
  370.8 4.3 copy-start.40
  381.5 12.2 %copy-start.19 = (bf16[1024,12,64]{0,2,1:T(8,128)(2,1)S(1)}, bf16[1024,12,64]{0,2,1:T(8,128)(2,1)}, u32[]{:S(2)}) copy-start(bf16[1024,12,64]{0,2,1:T(8,128)(2,1)} %get-tuple-element.525) | copy-start | bytes 4718596 | tf_op jit(solution)/shard_map/while/body/eval_jaxpr/while
  446.7 9.5 %copy-start.8 = (bf16[1024,12,64]{0,2,1:T(8,128)(2,1)S(1)}, bf16[1024,12,64]{0,2,1:T(8,128)(2,1)}, u32[]{:S(2)}) copy-start(bf16[1024,12,64]{0,2,1:T(8,128)(2,1)} %get-tuple-element.521) | copy-start | bytes 4718596 | tf_op jit(solution)/shard_map/while/body/eval_jaxpr/while
  468.4 11.5 %copy-start.19 = (bf16[1024,12,64]{0,2,1:T(8,128)(2,1)S(1)}, bf16[1024,12,64]{0,2,1:T(8,128)(2,1)}, u32[]{:S(2)}) copy-start(bf16[1024,12,64]{0,2,1:T(8,128)(2,1)} %get-tuple-element.525) | copy-start | bytes 4718596 | tf_op jit(solution)/shard_map/while/body/eval_jaxpr/while
  533.4 9.5 %copy-start.8 = (bf16[1024,12,64]{0,2,1:T(8,128)(2,1)S(1)}, bf16[1024,12,64]{0,2,1:T(8,128)(2,1)}, u32[]{:S(2)}) copy-start(bf16[1024,12,64]{0,2,1:T(8,128)(2,1)} %get-tuple-element.521) | copy-start | bytes 4718596 | tf_op jit(solution)/shard_map/while/body/eval_jaxpr/while
  557.0 6.6 copy-start.3
  567.5 6.0 copy-start.11
  567.5 6.0 copy-start.39
  567.5 6.0 copy-start.48
  567.5 6.0 copy-start.50
  567.6 6.0 copy-start.61
  606.8 3.0 copy-start.12
  606.8 3.8 copy-start.13
  610.6 3.5 copy-start.15
  610.6 4.0 copy-start.17
  610.6 4.0 copy-start.29
  610.6 4.0 copy-start.32
  610.6 4.0 copy-start.36
  610.6 3.9 copy-start.37
  610.6 3.9 copy-start.41
  610.6 3.9 copy-start.54
  618.4 239.2 %reduce-scatter.11.cloned.1.call-start = ((), (), s32[]{:S(2)}) async-start(), calls=%async_computation.11 | async-start | bytes 5308416 | tf_op jit(solution)/shard_map/reduce_scatter | solution.py:202
  639.5 5.0 copy-start.62
  639.6 5.5 copy-start.55
  639.6 5.5 copy-start.56
  639.6 5.5 copy-start.57
  639.6 249.4 %reduce-scatter.9.cloned.1.call-start = ((), (), s32[]{:S(2)}) async-start(), calls=%async_computation.10 | async-start | bytes 2433024 | tf_op jit(solution)/shard_map/reduce_scatter | solution.py:252
  652.8 3.7 copy-start.21
  (20 other events, 41.1 us)
Sparse Core Ops, SparseCore 0:
  11.8 62.7 all-gather.4
  77.5 52.6 all-gather.6
  618.5 237.2 all-reduce.5
Sparse Core Ops, SparseCore 1:
  169.6 51.5 all-gather.8
  222.6 44.7 all-gather.10
  311.2 56.4 reduce-scatter.6
  370.2 57.7 reduce-scatter.4
  639.6 129.5 reduce-scatter.10
  775.1 113.9 reduce-scatter.8
